TPU v7x, 256 devices: a whole 4x4x8 slice. The times are simulated.
256 devices in a mesh: row: 32 (over y, z), col: 8 (over x, core).
Axes of the slice: x: 4, y: 4, z: 8, core: 2. Of those that a mesh axis runs over, the one named last changes fastest.
Arguments:
- sim_window: bfloat16 [6144, 6144], P('row', 'col'), as said below
- sim_rest: bfloat16 [6144, 113856], P('row', 'col'), may hold values from -6 to 6
- joined_partner_pairs: int32 [768, 2], replicated, may hold values from 0 to 6143, as said below
- cluster_member_count: int32 [6144], replicated, may hold values from 1 to 64
Outputs:
- window_out: bfloat16 [6144, 6144], P('row', 'col')
- rest_out: bfloat16 [6144, 113856], P('row', 'col')
Inputs may be any that keep to these rules, and one draw needn't show every extreme that they name: `joined_partner_pairs`: each row is (survivor, partner); no window item appears twice in the whole list. Each aligned block of 192 items holds exactly 24 partners. For any two aligned blocks (possibly the same), at most 3 pairs have their partner in the first and their survivor in the second, and some two blocks have exactly 3. Nearly symmetric: sim_window[i, j] is close to sim_window[j, i].
All inputs are finite; a program needn't handle non-finite values.
Results may differ from a plain program's by a relative error of at most 0.001.
Values may be sent and summed in bfloat16 or wider, within the bound.
No kernel may reach another device: no remote copies, remote signals or barrier semaphores. Data moves between devices by JAX's collectives and lax.ppermute only.
A program may use at most 128 MiB of HBM per device.

v0:
```python
import jax
import jax.numpy as jnp
from jax import lax
from jax.sharding import PartitionSpec as P


def pairing_tables(joined_partner_pairs, cluster_member_count):
    lasting_node = joined_partner_pairs[:, 0]
    vanishing_node = joined_partner_pairs[:, 1]
    remaining_size = cluster_member_count[lasting_node].astype(jnp.float32)
    absorbed_size = cluster_member_count[vanishing_node].astype(jnp.float32)
    joined_cluster_size = remaining_size + absorbed_size
    return (
        lasting_node,
        vanishing_node,
        remaining_size / joined_cluster_size,
        absorbed_size / joined_cluster_size,
    )


def item_weight_values(node_labels, lasting_node, vanishing_node, retained_pair, selected_pair):
    lasting_mask = node_labels[:, None] == lasting_node[None, :]
    belongs_mask = node_labels[:, None] == vanishing_node[None, :]
    lasting_real_mask = lasting_mask.astype(jnp.float32)
    matched_mask = jnp.sum((lasting_mask | belongs_mask).astype(jnp.float32), axis=1)
    retained_entries = (
        1.0 - matched_mask + jnp.sum(lasting_real_mask * retained_pair[None, :], axis=1)
    )
    selected_entries = jnp.sum(lasting_real_mask * selected_pair[None, :], axis=1)
    donor_position = jnp.sum(jnp.where(lasting_mask, vanishing_node[None, :], 0), axis=1)
    return (retained_entries, selected_entries, donor_position)


def shards(sim_window, sim_rest, joined_partner_pairs, cluster_member_count):
    row_number_total = sim_window.shape[0]
    col_count = sim_window.shape[1]
    blocks = lax.axis_size("row")
    local_block = lax.axis_index("row")
    my_col = lax.axis_index("col")
    lasting_node, vanishing_node, retained_pair, selected_pair = pairing_tables(
        joined_partner_pairs, cluster_member_count
    )
    row_sequence = jnp.arange(row_number_total, dtype=jnp.int32)
    retained_entries, selected_entries, ignored = item_weight_values(
        local_block * row_number_total + row_sequence,
        lasting_node,
        vanishing_node,
        retained_pair,
        selected_pair,
    )
    src_block = vanishing_node // row_number_total
    destination_block = lasting_node // row_number_total
    pair_count = joined_partner_pairs.shape[0]
    pair_order = jnp.arange(pair_count, dtype=jnp.int32)
    earlier = pair_order[None, :] < pair_order[:, None]
    slot_width = row_number_total // 8
    same_route = src_block[None, :] == src_block[:, None]
    slot_rank = jnp.sum((earlier & same_route).astype(jnp.int32), axis=1)
    recv_slot = src_block * slot_width + slot_rank
    recv_width = blocks * slot_width
    mine_src = src_block == local_block
    slot_hot = (
        (jnp.arange(slot_width, dtype=jnp.int32)[:, None] == slot_rank[None, :]) & mine_src[None, :]
    ).astype(jnp.bfloat16)
    row_hot = (
        (vanishing_node - local_block * row_number_total)[:, None] == row_sequence[None, :]
    ).astype(jnp.bfloat16)
    selector = jnp.dot(slot_hot, row_hot, preferred_element_type=jnp.float32).astype(jnp.bfloat16)
    send_window = jnp.dot(selector, sim_window, preferred_element_type=jnp.float32).astype(
        jnp.bfloat16
    )
    send_rest = jnp.dot(selector, sim_rest, preferred_element_type=jnp.float32).astype(jnp.bfloat16)
    local_destination = destination_block == local_block
    target_hot = (
        ((lasting_node - local_block * row_number_total)[None, :] == row_sequence[:, None])
        & local_destination[None, :]
    ).astype(jnp.bfloat16)
    recv_hot = (recv_slot[:, None] == jnp.arange(recv_width, dtype=jnp.int32)[None, :]).astype(
        jnp.bfloat16
    )
    placement = jnp.dot(target_hot, recv_hot, preferred_element_type=jnp.float32).astype(
        jnp.bfloat16
    )
    placed_window = jnp.dot(
        placement,
        lax.all_gather(send_window, "row", axis=0, tiled=True),
        preferred_element_type=jnp.float32,
    )
    placed_rest = jnp.dot(
        placement,
        lax.all_gather(send_rest, "row", axis=0, tiled=True),
        preferred_element_type=jnp.float32,
    )
    mixed_window = (
        retained_entries[:, None] * sim_window.astype(jnp.float32)
        + selected_entries[:, None] * placed_window
    ).astype(jnp.bfloat16)
    rest_out = (
        retained_entries[:, None] * sim_rest.astype(jnp.float32)
        + selected_entries[:, None] * placed_rest
    ).astype(jnp.bfloat16)
    col_iota = jnp.arange(col_count, dtype=jnp.int32)
    column_identifiers = my_col * col_count + col_iota
    column_retained, column_selected, column_provider = item_weight_values(
        column_identifiers, lasting_node, vanishing_node, retained_pair, selected_pair
    )
    piece = lax.all_gather(mixed_window, "col", axis=1, tiled=True)
    piece_width = piece.shape[1]
    picker = (jnp.arange(piece_width, dtype=jnp.int32)[:, None] == column_provider[None, :]).astype(
        jnp.bfloat16
    )
    gathered = jnp.dot(piece, picker, preferred_element_type=jnp.float32)
    window_out = (
        column_retained[None, :] * mixed_window.astype(jnp.float32)
        + column_selected[None, :] * gathered
    ).astype(jnp.bfloat16)
    return (window_out, rest_out)


def solution(mesh):
    in_specs = (P("row", "col"), P("row", "col"), P(), P())
    out_specs = (P("row", "col"), P("row", "col"))
    return jax.shard_map(shards, mesh=mesh, in_specs=in_specs, out_specs=out_specs, check_vma=False)
```

profile of v0, /device:TPU:1, one launch (start us, length us, event | category | flops | bytes accessed | tf_op | source)
XLA Modules:
  0.0 313.5 jit_solution(18282270828736118344)
XLA Ops:
  7.2 0.0 copy-start
  7.2 0.0 all-gather.4.cloned.1.call-start
  7.2 0.8 fusion.32
  8.1 0.4 convert_reduce_fusion
  8.5 0.3 convolution_convert_fusion.2
  8.7 1.8 convolution_convert_fusion.1
  10.5 0.0 all-gather.4.cloned.1.call-update
  10.6 0.0 all-gather.6.cloned.1.call-start
  10.6 0.0 copy-done
  10.6 4.5 %gather_fusion = s32[768]{0:T(1024)S(1)} fusion(s32[6144]{0:T(1024)S(1)} %copy-done, s32[1024]{0:T(1024)S(1)} %get-tuple-element.25), kind=kCustom, calls=%fused_computation | custom fusion | bytes 9216 | tf_op jit(solution)/shard_map/gather | solution.py:10
  15.1 0.0 copy-start.2
  15.1 4.5 %gather_fusion.1 = s32[768]{0:T(1024)S(1)} fusion(s32[6144]{0:T(1024)S(1)} %copy-done, s32[1024]{0:T(1024)S(1)} %get-tuple-element.24), kind=kCustom, calls=%fused_computation.1 | custom fusion | bytes 9216 | tf_op jit(solution)/shard_map/gather | solution.py:11
  19.6 0.3 convert_reduce_fusion.2
  20.0 0.8 fusion.14
  20.8 65.7 %all-gather.4.cloned.1.call-done = bf16[768,768]{1,0:T(8,128)(2,1)} async-done(((bf16[24,768]{1,0:T(8,128)(2,1)}), bf16[768,768]{1,0:T(8,128)(2,1)}) %all-gather.4.cloned.1.call-update) | async-done | bytes 1179664 | tf_op jit(solution)/shard_map/all_gather | solution.py:86
  86.5 0.0 copy-done.2
  86.5 2.4 fusion.13
  88.9 0.0 all-gather.6.cloned.1.call-update
  88.9 0.0 copy-start.1
  88.9 0.2 all-gather.8.cloned.1.call-start
  89.1 4.3 %convolution_convert_fusion = bf16[24,14232]{1,0:T(8,128)(2,1)} fusion(bf16[24,192]{1,0:T(8,128)(2,1)S(1)} %convolution_convert_fusion.2, bf16[192,14232]{1,0:T(8,128)(2,1)} %param.5), kind=kOutput, calls=%fused_computation.7 | convolution fusion | flops 131503680 | bytes 6157440 | tf_op jit(solution)/shard_map/dot_general | solution.py:72
  93.4 0.0 all-gather.8.cloned.1.call-update
  93.4 0.4 fusion.6
  93.8 0.9 convert_reduce_fusion.1
  94.7 25.4 %all-gather.6.cloned.1.call-done = bf16[192,6144]{1,0:T(8,128)(2,1)} async-done(((bf16[192,768]{1,0:T(8,128)(2,1)}), bf16[192,6144]{1,0:T(8,128)(2,1)}) %all-gather.6.cloned.1.call-update) | async-done | bytes 2359312 | tf_op jit(solution)/shard_map/all_gather | solution.py:107
  120.1 0.0 copy-done.1
  120.1 6.4 %fusion.12 = bf16[192,768]{1,0:T(8,128)(2,1)} fusion(bf16[192,6144]{1,0:T(8,128)(2,1)} %all-gather.6.cloned.1.call-done, s32[768]{0:T(1024)S(1)} %fusion.6, bf16[192,768]{1,0:T(8,128)(2,1)S(1)} %copy-done.1, f32[768]{0:T(1024)S(1)} %get-tuple-element.3, f32[768]{0:T(1024)S(1)} %subtract_add_fusion), kind=kOutput, calls=%fused_computation.26 | convolution fusion | flops 1817395200 | bytes 2958336 | tf_op jit(solution)/shard_map/dot_general | solution.py:112
  126.5 162.6 %all-gather.8.cloned.1.call-done = bf16[768,14232]{1,0:T(8,128)(2,1)} async-done(((bf16[24,14232]{1,0:T(8,128)(2,1)}), bf16[768,14232]{1,0:T(8,128)(2,1)}) %all-gather.8.cloned.1.call-update) | async-done | bytes 21860368 | tf_op jit(solution)/shard_map/all_gather | solution.py:91
  289.1 17.9 %fusion.2 = bf16[192,14232]{1,0:T(8,128)(2,1)} fusion(bf16[192,768]{1,0:T(8,128)(2,1)S(1)} %fusion.14, bf16[768,14232]{1,0:T(8,128)(2,1)} %all-gather.8.cloned.1.call-done, bf16[192,14232]{1,0:T(8,128)(2,1)} %param.5, f32[192]{0:T(256)S(1)} %get-tuple-element.12, f32[192]{0:T(256)S(1)} %subtract_add_fusion.1), kind=kOutput, calls=%fused_computation.6 | convolution fusion | flops 4210850304 | bytes 33086976 | tf_op jit(solution)/shard_map/dot_general | solution.py:89
  (10 shorter events, 0.1 us)
Async XLA Ops:
  7.2 3.5 %copy-start = (s32[6144]{0:T(1024)S(1)}, s32[6144]{0:T(1024)}, u32[]{:S(2)}) copy-start(s32[6144]{0:T(1024)} %param.7) | copy-start | bytes 73732
  7.2 79.3 %all-gather.4.cloned.1.call-start = ((), (), s32[]{:S(2)}) async-start(), calls=%async_computation | async-start | bytes 1216512 | tf_op jit(solution)/shard_map/all_gather | solution.py:86
  10.6 109.6 %all-gather.6.cloned.1.call-start = ((), (), s32[]{:S(2)}) async-start(), calls=%async_computation.1 | async-start | bytes 2654208 | tf_op jit(solution)/shard_map/all_gather | solution.py:107
  15.1 71.4 %copy-start.2 = (bf16[192,768]{1,0:T(8,128)(2,1)S(1)}, bf16[192,768]{1,0:T(8,128)(2,1)}, u32[]{:S(2)}) copy-start(bf16[192,768]{1,0:T(8,128)(2,1)} %param.4) | copy-start | bytes 884740
  88.9 31.2 %copy-start.1 = (bf16[192,768]{1,0:T(8,128)(2,1)S(1)}, bf16[192,768]{1,0:T(8,128)(2,1)}, u32[]{:S(2)}) copy-start(bf16[192,768]{1,0:T(8,128)(2,1)} %fusion.13) | copy-start | bytes 884740
  88.9 200.2 %all-gather.8.cloned.1.call-start = ((), (), s32[]{:S(2)}) async-start(), calls=%async_computation.2 | async-start | bytes 22708224 | tf_op jit(solution)/shard_map/all_gather | solution.py:91
Sparse Core Ops, SparseCore 0:
  11.1 75.2 all-gather.3
  89.0 31.0 all-gather.5
  123.3 165.8 all-gather.7
where the time goes:
time: 314 us
  waiting for transfers between devices  254 us (81%)
  matrix products  33.7 us (11%)
  between operations  13.9 us (4%)
  local copies, waits for them, and re-layouts  8.95 us (3%)
    all_gather x1, waiting for transfers between devices, shards(): lax.all_gather(send_rest, 'row', axis=0, tiled=True)  163 us
    all_gather x1, waiting for transfers between devices, shards(): lax.all_gather(send_window, 'row', axis=0, tiled=True)  65.7 us
    all_gather x1, waiting for transfers between devices, shards(): piece = lax.all_gather(mixed_window, 'col', axis=1, tiled=True)  25.4 us
    dot_general x1, matrix products, shards(): jnp.dot(placement, lax.all_gather(send_rest, 'row', axis=0, tiled=True),...  17.9 us
    dot_general x1, matrix products, shards(): gathered = jnp.dot(piece, picker, preferred_element_type=jnp.float32)  6.39 us
  transfers between devices with their start and end apart: 3, of which 3 were waited for; matrix products, arithmetic and copies ran while one was open for 7% of the time, Pallas kernels for 0%

commit v1 on v0

--- a/solution.py
+++ b/solution.py
@@ -2,6 +2,24 @@
 import jax.numpy as jnp
 from jax import lax
 from jax.sharding import PartitionSpec as P
+
+
+def ring_gather(value, axis, dim):
+    ways, here, turn = (lax.axis_size(axis), lax.axis_index(axis), value.shape[dim])
+    dims = [n * ways if d == dim else n for d, n in enumerate(value.shape)]
+    full = lax.dynamic_update_slice_in_dim(
+        jnp.zeros(dims, value.dtype), value, here * turn, axis=dim
+    )
+    going_up = going_down = value
+    for far in range(1, ways // 2 + 1):
+        going_up = lax.ppermute(going_up, axis, [(d, (d + 1) % ways) for d in range(ways)])
+        full = lax.dynamic_update_slice_in_dim(full, going_up, (here - far) % ways * turn, axis=dim)
+        if 2 * far < ways:
+            going_down = lax.ppermute(going_down, axis, [(d, (d - 1) % ways) for d in range(ways)])
+            full = lax.dynamic_update_slice_in_dim(
+                full, going_down, (here + far) % ways * turn, axis=dim
+            )
+    return full
 
 
 def pairing_tables(joined_partner_pairs, cluster_member_count):
@@ -104,7 +122,7 @@
     column_retained, column_selected, column_provider = item_weight_values(
         column_identifiers, lasting_node, vanishing_node, retained_pair, selected_pair
     )
-    piece = lax.all_gather(mixed_window, "col", axis=1, tiled=True)
+    piece = ring_gather(mixed_window, "col", 1)
     piece_width = piece.shape[1]
     picker = (jnp.arange(piece_width, dtype=jnp.int32)[:, None] == column_provider[None, :]).astype(
         jnp.bfloat16

time: 314 us -> 282 us (0.90)
  waiting for transfers between devices: 254 us -> 206 us
  starting transfers between devices: 0.3 us -> 15.4 us
  local copies, waits for them, and re-layouts: 8.95 us -> 13.3 us
  matrix products: 33.7 us -> 29.4 us
    all_gather x1, waiting for transfers between devices: 163 us -> 135 us  [shards(): lax.all_gather(send_rest, 'row', axis=0, tiled=True)]
    all_gather x1 -> x0, waiting for transfers between devices: 25.4 us -> none  [shards(): piece = lax.all_gather(mixed_window, 'col', axis=1, tiled=True)]
    ppermute x0 -> x7, starting transfers between devices: none -> 15.4 us  [the longest x4 13.8 us: ring_gather(): lax.ppermute(going_up, axis, [(d, (d + 1) % ways) for d in range(ways)])]
    ppermute x0 -> x7, waiting for transfers between devices: none -> 9.62 us  [the longest x4 7.49 us: ring_gather(): lax.ppermute(going_up, axis, [(d, (d + 1) % ways) for d in range(ways)])]
    all_gather x1, waiting for transfers between devices: 65.7 us -> 61.4 us  [shards(): lax.all_gather(send_window, 'row', axis=0, tiled=True)]
  transfers between devices with their start and end apart: 3 -> 9, of which waited for: 3 -> 6; matrix products, arithmetic and copies ran while one was open for 7% -> 9% of each run, Pallas kernels for 0% -> 0%
where the time goes in v1:
time: 282 us
  waiting for transfers between devices  206 us (73%)
  matrix products  29.4 us (10%)
  starting transfers between devices  15.4 us (5%)
  between operations  14.4 us (5%)
  local copies, waits for them, and re-layouts  13.3 us (5%)
  other arithmetic  2.9 us (1%)
    all_gather x1, waiting for transfers between devices, shards(): lax.all_gather(send_rest, 'row', axis=0, tiled=True)  135 us
    all_gather x1, waiting for transfers between devices, shards(): lax.all_gather(send_window, 'row', axis=0, tiled=True)  61.4 us
    dot_general x1, matrix products, shards(): jnp.dot(placement, lax.all_gather(send_rest, 'row', axis=0, tiled=True),...  17.2 us
    ppermute x4, starting transfers between devices, ring_gather(): lax.ppermute(going_up, axis, [(d, (d + 1) % ways) for d in range(ways)])  13.8 us
    ppermute x4, waiting for transfers between devices, ring_gather(): lax.ppermute(going_up, axis, [(d, (d + 1) % ways) for d in range(ways)])  7.49 us
  transfers between devices with their start and end apart: 9, of which 6 were waited for; matrix products, arithmetic and copies ran while one was open for 9% of the time, Pallas kernels for 0%

profile of v1, /device:TPU:1, one launch (start us, length us, event | category | flops | bytes accessed | tf_op | source)
XLA Modules:
  0.0 281.9 jit_solution(4324352239070329332)
XLA Ops:
  7.2 0.8 fusion.32
  8.1 0.4 convert_reduce_fusion
  8.5 0.3 convolution_convert_fusion.2
  8.7 1.8 convolution_convert_fusion.1
  10.6 0.0 all-gather.5.cloned.1.call-start
  10.6 4.3 %convolution_convert_fusion = bf16[24,14232]{1,0:T(8,128)(2,1)} fusion(bf16[24,192]{1,0:T(8,128)(2,1)S(1)} %convolution_convert_fusion.2, bf16[192,14232]{1,0:T(8,128)(2,1)} %param.5), kind=kOutput, calls=%fused_computation.7 | convolution fusion | flops 131503680 | bytes 6157440 | tf_op jit(solution)/shard_map/dot_general | solution.py:90
  14.9 4.5 %gather_fusion = s32[768]{0:T(1024)S(1)} fusion(s32[6144]{0:T(1024)S(1)} %copy-done, s32[1024]{0:T(1024)S(1)} %get-tuple-element.27), kind=kCustom, calls=%fused_computation | custom fusion | bytes 9216 | tf_op jit(solution)/shard_map/gather | solution.py:28
  19.4 4.5 %gather_fusion.1 = s32[768]{0:T(1024)S(1)} fusion(s32[6144]{0:T(1024)S(1)} %copy-done, s32[1024]{0:T(1024)S(1)} %get-tuple-element.26), kind=kCustom, calls=%fused_computation.1 | custom fusion | bytes 9216 | tf_op jit(solution)/shard_map/gather | solution.py:29
  23.9 0.3 convert_reduce_fusion.2
  24.3 0.8 fusion.14
  25.0 61.4 %all-gather.3.cloned.1.call-done = bf16[768,768]{1,0:T(8,128)(2,1)} async-done(((bf16[24,768]{1,0:T(8,128)(2,1)}), bf16[768,768]{1,0:T(8,128)(2,1)}) %all-gather.3.cloned.1.call-update) | async-done | bytes 1179664 | tf_op jit(solution)/shard_map/all_gather | solution.py:104
  86.5 0.2 broadcast_in_dim.8
  86.7 1.0 copy-done.2
  87.8 0.4 constant_dynamic-update-slice_fusion.7
  88.2 6.8 %collective-permute-start = (bf16[192,768]{1,0:T(8,128)(2,1)S(1)}, bf16[192,768]{1,0:T(8,128)(2,1)}, u32[]{:S(2)}, u32[]{:S(2)}) collective-permute-start(bf16[192,768]{1,0:T(8,128)(2,1)S(1)} %get-tuple-element.25), channel_id=1, source_target_pairs={{0,1},{1,2},{2,3},{3,4},{4,5},{5,6},{6,7},{7,0},{8,9},{9,10},{10,1... | collective-permute-start | bytes 884744 | tf_op jit(solution)/shard_map/ppermute | solution.py:15
  95.0 0.9 convert_reduce_fusion.1
  95.9 2.7 collective-permute-done
  98.6 2.6 collective-permute-start.2
  101.2 0.2 collective-permute-start.3
  101.4 0.4 fusion.6
  101.9 3.3 %collective-permute-done.2 = bf16[192,768]{1,0:T(8,128)(2,1)} collective-permute-done((bf16[192,768]{1,0:T(8,128)(2,1)}, bf16[192,768]{1,0:T(8,128)(2,1)}, u32[]{:S(2)}, u32[]{:S(2)}) %collective-permute-start.2) | collective-permute-done | bytes 294944 | tf_op jit(solution)/shard_map/ppermute | solution.py:15
  105.2 2.5 collective-permute-start.4
  107.7 1.0 constant_dynamic-update-slice_fusion.6
  108.7 1.0 constant_dynamic-update-slice_fusion.5
  109.7 1.4 collective-permute-start.5
  111.1 1.0 constant_dynamic-update-slice_fusion.4
  112.1 2.0 collective-permute-start.6
  114.1 2.1 collective-permute-done.5
  116.3 1.4 collective-permute-done.6
  117.7 4.7 %fusion.12 = bf16[192,768]{1,0:T(8,128)(2,1)} fusion(bf16[192,6144]{1,0:T(8,128)(2,1)S(1)} %constant_dynamic-update-slice_fusion, s32[768]{0:T(1024)S(1)} %fusion.6, bf16[192,768]{1,0:T(8,128)(2,1)S(1)} %get-tuple-element.25, f32[768]{0:T(1024)S(1)} %get-tuple-element.3, f32[768]{0:T(1024)S(1)} %subtract_add_fusion), kind=kOutput, calls=%fused_computation.26 | convolution fusion | flops 1817395200 | bytes 2958336 | tf_op jit(solution)/shard_map/dot_general | solution.py:130
  122.4 135.4 %all-gather.5.cloned.1.call-done = bf16[768,14232]{1,0:T(8,128)(2,1)} async-done(((bf16[24,14232]{1,0:T(8,128)(2,1)}), bf16[768,14232]{1,0:T(8,128)(2,1)}) %all-gather.5.cloned.1.call-update) | async-done | bytes 21860368 | tf_op jit(solution)/shard_map/all_gather | solution.py:109
  257.8 17.2 %fusion.2 = bf16[192,14232]{1,0:T(8,128)(2,1)} fusion(bf16[192,768]{1,0:T(8,128)(2,1)S(1)} %fusion.14, bf16[768,14232]{1,0:T(8,128)(2,1)} %all-gather.5.cloned.1.call-done, bf16[192,14232]{1,0:T(8,128)(2,1)} %param.5, f32[192]{0:T(256)S(1)} %get-tuple-element.12, f32[192]{0:T(256)S(1)} %subtract_add_fusion.1), kind=kOutput, calls=%fused_computation.6 | convolution fusion | flops 4210850304 | bytes 33086976 | tf_op jit(solution)/shard_map/dot_general | solution.py:107
  (26 shorter events, 0.3 us)
Async XLA Ops:
  7.2 7.7 %copy-start = (s32[6144]{0:T(1024)S(1)}, s32[6144]{0:T(1024)}, u32[]{:S(2)}) copy-start(s32[6144]{0:T(1024)} %param.7) | copy-start | bytes 73732
  7.2 79.3 %all-gather.3.cloned.1.call-start = ((), (), s32[]{:S(2)}) async-start(), calls=%async_computation | async-start | bytes 1216512 | tf_op jit(solution)/shard_map/all_gather | solution.py:104
  10.6 247.3 %all-gather.5.cloned.1.call-start = ((), (), s32[]{:S(2)}) async-start(), calls=%async_computation.1 | async-start | bytes 22708224 | tf_op jit(solution)/shard_map/all_gather | solution.py:109
  23.8 62.9 %copy-start.1 = (bf16[192,768]{1,0:T(8,128)(2,1)S(1)}, bf16[192,768]{1,0:T(8,128)(2,1)}, u32[]{:S(2)}) copy-start(bf16[192,768]{1,0:T(8,128)(2,1)} %param.4) | copy-start | bytes 884740
  86.5 1.3 copy-start.2
  88.2 10.5 %collective-permute-start = (bf16[192,768]{1,0:T(8,128)(2,1)S(1)}, bf16[192,768]{1,0:T(8,128)(2,1)}, u32[]{:S(2)}, u32[]{:S(2)}) collective-permute-start(bf16[192,768]{1,0:T(8,128)(2,1)S(1)} %get-tuple-element.25), channel_id=1, source_target_pairs={{0,1},{1,2},{2,3},{3,4},{4,5},{5,6},{6,7},{7,0},{8,9},{9,10},{10,1... | collective-permute-start | bytes 884744 | tf_op jit(solution)/shard_map/ppermute | solution.py:15
  95.0 6.3 %collective-permute-start.1 = (bf16[192,768]{1,0:T(8,128)(2,1)S(1)}, bf16[192,768]{1,0:T(8,128)(2,1)}, u32[]{:S(2)}, u32[]{:S(2)}) collective-permute-start(bf16[192,768]{1,0:T(8,128)(2,1)S(1)} %get-tuple-element.25), channel_id=1, source_target_pairs={{0,7},{1,0},{2,1},{3,2},{4,3},{5,4},{6,5},{7,6},{8,15},{9,8},{10,9... | collective-permute-start | bytes 884744 | tf_op jit(solution)/shard_map/ppermute | solution.py:18
  98.6 6.6 %collective-permute-start.2 = (bf16[192,768]{1,0:T(8,128)(2,1)}, bf16[192,768]{1,0:T(8,128)(2,1)}, u32[]{:S(2)}, u32[]{:S(2)}) collective-permute-start(bf16[192,768]{1,0:T(8,128)(2,1)} %collective-permute-done), channel_id=1, source_target_pairs={{0,1},{1,2},{2,3},{3,4},{4,5},{5,6},{6,7},{7,0},{8,9},{9,10},{10,1... | collective-permute-start | bytes 884744 | tf_op jit(solution)/shard_map/ppermute | solution.py:15
  101.2 8.5 %collective-permute-start.3 = (bf16[192,768]{1,0:T(8,128)(2,1)}, bf16[192,768]{1,0:T(8,128)(2,1)S(1)}, u32[]{:S(2)}, u32[]{:S(2)}) collective-permute-start(bf16[192,768]{1,0:T(8,128)(2,1)} %collective-permute-done.1), channel_id=1, source_target_pairs={{0,7},{1,0},{2,1},{3,2},{4,3},{5,4},{6,5},{7,6},{8,15},{9,8},{10,9... | collective-permute-start | bytes 884744 | tf_op jit(solution)/shard_map/ppermute | solution.py:18
  105.2 6.9 %collective-permute-start.4 = (bf16[192,768]{1,0:T(8,128)(2,1)}, bf16[192,768]{1,0:T(8,128)(2,1)S(1)}, u32[]{:S(2)}, u32[]{:S(2)}) collective-permute-start(bf16[192,768]{1,0:T(8,128)(2,1)} %collective-permute-done.2), channel_id=1, source_target_pairs={{0,1},{1,2},{2,3},{3,4},{4,5},{5,6},{6,7},{7,0},{8,9},{9,10},{10,1... | collective-permute-start | bytes 884744 | tf_op jit(solution)/shard_map/ppermute | solution.py:15
  109.7 6.6 %collective-permute-start.5 = (bf16[192,768]{1,0:T(8,128)(2,1)S(1)}, bf16[192,768]{1,0:T(8,128)(2,1)S(1)}, u32[]{:S(2)}, u32[]{:S(2)}) collective-permute-start(bf16[192,768]{1,0:T(8,128)(2,1)S(1)} %collective-permute-done.3), channel_id=1, source_target_pairs={{0,7},{1,0},{2,1},{3,2},{4,3},{5,4},{6,5},{7,6},{8,15},{9,8},{10,9... | collective-permute-start | bytes 884744 | tf_op jit(solution)/shard_map/ppermute | solution.py:18
  112.1 5.6 %collective-permute-start.6 = (bf16[192,768]{1,0:T(8,128)(2,1)S(1)}, bf16[192,768]{1,0:T(8,128)(2,1)S(1)}, u32[]{:S(2)}, u32[]{:S(2)}) collective-permute-start(bf16[192,768]{1,0:T(8,128)(2,1)S(1)} %collective-permute-done.4), channel_id=1, source_target_pairs={{0,1},{1,2},{2,3},{3,4},{4,5},{5,6},{6,7},{7,0},{8,9},{9,10},{10,1... | collective-permute-start | bytes 884744 | tf_op jit(solution)/shard_map/ppermute | solution.py:15
Sparse Core Ops, SparseCore 0:
  11.1 75.2 all-gather.2
  89.6 168.1 all-gather.4
